TPU v7x, 256 devices: a 4x2x16 block of a 4x16x16 slice. The times are simulated.
256 devices in a mesh: parts: 2 (over y), row: 128 (over z, x, core).
Axes of the slice: x: 4, y: 2, z: 16, core: 2. Of those that a mesh axis runs over, the one named last changes fastest.
The devices are a block of a 4x16x16 slice.
Arguments:
- tokens: bfloat16 [512, 256, 768], P(('parts', 'row')), parts along dimension 0, may hold values from -6 to 6
- w_query: bfloat16 [768, 768], replicated, may hold values from -0.21875 to 0.21875
- w_key: bfloat16 [768, 768], replicated, may hold values from -0.21875 to 0.21875
- w_value: bfloat16 [768, 768], replicated, may hold values from -0.21875 to 0.21875
- w_out: bfloat16 [768, 768], replicated, may hold values from -0.21875 to 0.21875
- omega: bfloat16 [12, 64, 256], replicated, may hold values from -5 to 5
- conv_kernel: float32 [3, 3, 768], replicated, may hold values from -0.6 to 0.6
- norm_gain: float32 [768], replicated, may hold values from 0.1 to 1.9
Outputs:
- layer_out: bfloat16 [512, 256, 768], P(('parts', 'row')), parts along dimension 0
There are 2 independent parts, one for each index of `parts`. A program takes and returns all parts, laid end to end along the dimension named above; an argument that names none is the same for every part. Nothing has to cross between parts.
All inputs are finite; a program needn't handle non-finite values.
Results may differ from a plain program's by a relative error of at most 0.0081.
Values may be sent and summed in bfloat16 or wider, within the bound.
A program may use at most 64 MiB of HBM per device.

v0:
```python
import jax
import jax.numpy as jnp
from jax import lax
from jax.sharding import PartitionSpec as P


def with_halo(block, sides, width):
    for axis, dim in sides:
        count = lax.axis_size(axis)
        forward = [(i, i + 1) for i in range(count - 1)]
        backward = [(target, source) for source, target in forward]
        low = lax.ppermute(
            lax.slice_in_dim(block, block.shape[dim] - width, None, axis=dim), axis, forward
        )
        high = lax.ppermute(lax.slice_in_dim(block, 0, width, axis=dim), axis, backward)
        block = jnp.concatenate([low, block, high], axis=dim)
    return block


def packed_total(arrays, axis):
    ends = [0]
    for a in arrays:
        ends.append(ends[-1] + a.size)
    subtotal = lax.psum(jnp.concatenate([a.ravel() for a in arrays]), axis)
    return tuple((subtotal[b:e].reshape(a.shape) for a, b, e in zip(arrays, ends, ends[1:])))


def project(rows, weight):
    return jnp.dot(rows, weight, preferred_element_type=jnp.float32).astype(jnp.bfloat16)


def feature_map(heads_in, omega):
    dim_head = heads_in.shape[-1]
    lifted = jnp.einsum("thd,hdf->thf", heads_in, omega, preferred_element_type=jnp.float32)
    values = heads_in.astype(jnp.float32)
    square = jnp.sum(values * values, axis=-1, keepdims=True)
    feats = jnp.exp(lifted * dim_head ** (-0.25) - square * 0.5 * dim_head ** (-0.5)) * omega.shape[
        -1
    ] ** (-0.5)
    return feats.astype(jnp.bfloat16)


def shards(tokens, w_query, w_key, w_value, w_out, omega, conv_kernel, norm_gain):
    rows_here, cols, width = tokens.shape
    heads, dim_head, nfeat = omega.shape
    flat = tokens.reshape(rows_here * cols, width)
    value = project(flat, w_value)
    value_ext = with_halo(value.reshape(rows_here, cols, width), (("row", 0),), 1)
    feat_key = feature_map(project(flat, w_key).reshape(-1, heads, dim_head), omega)
    local_state = jnp.einsum(
        "thf,thd->fhd",
        feat_key,
        value.reshape(-1, heads, dim_head),
        preferred_element_type=jnp.float32,
    )
    local_sum = jnp.sum(feat_key.astype(jnp.float32), axis=0)
    feat_query = feature_map(project(flat, w_query).reshape(-1, heads, dim_head), omega)
    padded = jnp.pad(value_ext.astype(jnp.float32), ((0, 0), (1, 1), (0, 0)))
    position = jnp.zeros((rows_here, cols, width), jnp.float32)
    for shift_a in range(3):
        for shift_b in range(3):
            position = (
                position
                + padded[shift_a : shift_a + rows_here, shift_b : shift_b + cols, :]
                * conv_kernel[shift_a, shift_b]
            )
    kv_sum, key_sum = packed_total((local_state.reshape(nfeat, width), local_sum), "row")
    kv_state = kv_sum.astype(jnp.bfloat16).reshape(nfeat, heads, dim_head)
    numer = jnp.einsum("thf,fhd->thd", feat_query, kv_state, preferred_element_type=jnp.float32)
    denom = jnp.einsum("thf,hf->th", feat_query.astype(jnp.float32), key_sum)
    attn = numer / denom[:, :, None]
    scale = lax.rsqrt(jnp.mean(attn * attn, axis=(1, 2), keepdims=True) + 1e-06)
    normed = (attn * scale).reshape(-1, width) * norm_gain
    mixed = (normed + position.reshape(-1, width)).astype(jnp.bfloat16)
    out = flat.astype(jnp.float32) + jnp.dot(mixed, w_out, preferred_element_type=jnp.float32)
    return out.astype(jnp.bfloat16).reshape(rows_here, cols, width)


def solution(mesh):
    return jax.shard_map(
        shards,
        mesh=mesh,
        in_specs=(P(("parts", "row"), None, None), P(), P(), P(), P(), P(), P(), P()),
        out_specs=P(("parts", "row"), None, None),
        check_vma=False,
    )
```

profile of v0, /device:TPU:33, one launch (start us, length us, event | category | flops | bytes accessed | tf_op | source)
XLA Modules:
  0.0 389.6 jit_solution(8754632436794415940)
XLA Ops:
  6.5 0.0 copy-start
  6.6 0.0 all-reduce.3.cloned.1.call-start
  6.6 1.3 copy-done
  7.8 1.9 convolution_convert_fusion.1
  9.7 0.3 copy.14
  10.0 0.2 multiply_reduce_fusion.2
  10.2 0.6 broadcast_multiply_fusion.2
  10.8 2.3 convolution_convert_fusion.2
  13.1 0.0 copy-start.1
  13.1 0.3 copy.13
  13.4 3.3 convert_reduce_fusion
  16.7 0.0 copy-done.1
  16.7 1.5 convolution_bitcast_fusion
  18.2 2.4 copy.15
  20.7 1.2 reshape_reshape.3
  21.9 0.0 copy-start.2
  21.9 2.2 pad_maximum_fusion
  24.0 0.0 copy-start.5
  24.0 0.1 all-reduce.3.cloned.1.call-update
  24.1 0.0 copy-done.2
  24.1 0.9 slice_bitcast_fusion.1
  25.0 4.6 %collective-permute-start = (bf16[1,256,768]{2,1,0:T(8,128)(2,1)}, bf16[1,256,768]{2,1,0:T(8,128)(2,1)}, u32[]{:S(2)}, u32[]{:S(2)}) collective-permute-start(bf16[1,256,768]{2,1,0:T(8,128)(2,1)} %get-tuple-element.14), channel_id=1, source_target_pairs={{0,1},{1,2},{2,3},{3,4},{4,5},{5,6},{6,7},{7,8},{8,9},{9,10},{10,1... | collective-permute-start | bytes 1179656 | tf_op jit(solution)/shard_map/ppermute | solution.py:12
  29.6 20.0 %collective-permute-start.1 = (bf16[1,256,768]{2,1,0:T(8,128)(2,1)}, bf16[1,256,768]{2,1,0:T(8,128)(2,1)}, u32[]{:S(2)}, u32[]{:S(2)}) collective-permute-start(bf16[1,256,768]{2,1,0:T(8,128)(2,1)} %get-tuple-element.15), channel_id=1, source_target_pairs={{1,0},{2,1},{3,2},{4,3},{5,4},{6,5},{7,6},{8,7},{9,8},{10,9},{11,1... | collective-permute-start | bytes 1179656 | tf_op jit(solution)/shard_map/ppermute | solution.py:15
  49.6 0.0 copy-done.5
  49.6 2.0 convolution_convert_fusion
  51.7 0.3 copy.16
  52.0 0.2 multiply_reduce_fusion.1
  52.2 0.9 slice_reduce_fusion.8
  53.1 4.1 %fusion.2 = bf16[512,12,256]{2,0,1:T(8,128)(2,1)} fusion(f32[512,12]{0,1:T(8,128)S(1)} %broadcast_multiply_fusion.1, bf16[512,12,64]{0,2,1:T(8,128)(2,1)S(1)} %bitcast.64, bf16[12,64,256]{2,1,0:T(8,128)(2,1)} %param.13), kind=kOutput, calls=%fused_computation.3 | convolution fusion | flops 207618048 | bytes 4349952 | tf_op jit(solution)/shard_map/thd,hdf->thf/dot_general | solution.py:34
  57.3 0.0 collective-permute-done
  57.3 0.0 collective-permute-done.1
  57.3 1.4 maximum_convert_fusion
  58.6 2.5 fusion.14
  61.1 1.9 copy.18
  63.0 306.4 %all-reduce.3.cloned.1.call-done = f32[199680]{0:T(1024)} async-done(((f32[199680]{0:T(1024)}), f32[199680]{0:T(1024)}) %all-reduce.3.cloned.1.call-update) | async-done | bytes 798736 | tf_op jit(solution)/shard_map/psum | solution.py:24
  369.4 0.7 slice.120
  370.1 2.8 fusion.23
  372.9 1.2 slice.191
  374.1 1.4 reshape.74
  375.5 3.3 multiply_reduce_fusion
  378.9 0.0 copy-start.3
  378.9 0.2 broadcast_multiply_fusion
  379.1 0.5 copy-done.3
  379.6 0.0 copy-start.4
  379.6 0.0 copy-start.6
  379.6 0.3 fusion.21
  379.8 1.0 copy-done.4
  380.8 0.2 copy-done.6
  381.1 1.7 add_convert_fusion
  (4 shorter events, 0.0 us)
Async XLA Ops:
  6.5 1.3 copy-start
  6.6 362.9 %all-reduce.3.cloned.1.call-start = ((), (), s32[]{:S(2)}) async-start(), calls=%async_computation | async-start | bytes 1597440 | tf_op jit(solution)/shard_map/psum | solution.py:24
  13.1 3.6 copy-start.1
  21.9 2.2 copy-start.2
  24.0 25.6 %copy-start.5 = (bf16[2,256,768]{2,1,0:T(8,128)(2,1)S(1)}, bf16[2,256,768]{2,1,0:T(8,128)(2,1)}, u32[]{:S(2)}) copy-start(bf16[2,256,768]{2,1,0:T(8,128)(2,1)} %param.8) | copy-start | bytes 2359300
  25.0 32.2 %collective-permute-start = (bf16[1,256,768]{2,1,0:T(8,128)(2,1)}, bf16[1,256,768]{2,1,0:T(8,128)(2,1)}, u32[]{:S(2)}, u32[]{:S(2)}) collective-permute-start(bf16[1,256,768]{2,1,0:T(8,128)(2,1)} %get-tuple-element.14), channel_id=1, source_target_pairs={{0,1},{1,2},{2,3},{3,4},{4,5},{5,6},{6,7},{7,8},{8,9},{9,10},{10,1... | collective-permute-start | bytes 1179656 | tf_op jit(solution)/shard_map/ppermute | solution.py:12
  29.6 27.6 %collective-permute-start.1 = (bf16[1,256,768]{2,1,0:T(8,128)(2,1)}, bf16[1,256,768]{2,1,0:T(8,128)(2,1)}, u32[]{:S(2)}, u32[]{:S(2)}) collective-permute-start(bf16[1,256,768]{2,1,0:T(8,128)(2,1)} %get-tuple-element.15), channel_id=1, source_target_pairs={{1,0},{2,1},{3,2},{4,3},{5,4},{6,5},{7,6},{8,7},{9,8},{10,9},{11,1... | collective-permute-start | bytes 1179656 | tf_op jit(solution)/shard_map/ppermute | solution.py:15
  378.9 0.7 copy-start.3
  379.6 1.3 copy-start.4
  379.6 1.5 copy-start.6
Sparse Core Ops, SparseCore 0:
  24.2 345.1 all-reduce.2
where the time goes:
time: 390 us
  waiting for transfers between devices  306 us (78%)
  starting transfers between devices  24.6 us (6%)
  matrix products  23 us (6%)
  local copies, waits for them, and re-layouts  14.5 us (4%)
  between operations  13.6 us (3%)
  other arithmetic  7.49 us (2%)
    psum x1, waiting for transfers between devices, packed_total(): subtotal = lax.psum(jnp.concatenate([a.ravel() for a in arrays]), axis)  306 us
    ppermute x1, starting transfers between devices, with_halo(): lax.ppermute(lax.slice_in_dim(block, 0, width, axis=dim), axis, backward)  20 us
  transfers between devices with their start and end apart: 3, of which 1 were waited for; matrix products, arithmetic and copies ran while one was open for 4% of the time, Pallas kernels for 0%

commit v1 on v0

v1 whole, which is shorter than its diff:
```python
import functools
import math

import jax
import jax.numpy as jnp
from jax import lax
from jax.experimental import pallas as pl
from jax.experimental.pallas import tpu as pltpu
from jax.sharding import PartitionSpec as P

MESH = pl.DeviceIdType.MESH
F32 = jnp.float32
BF16 = jnp.bfloat16

XS = 4
ZN = 4
CORES = 2
NEAR = XS * ZN
KV_ROWS = 48
CHUNK = 64


def near_peer(zl, x, a, b):
    if a == 0:
        zp = zl
    elif a == 1:
        zp = zl + 1 - 2 * (zl % 2)
    elif a == 2:
        zp = (zl + 2) % 4
    else:
        zp = 3 - zl
    return zp * XS + (x + b) % XS


STEPS = [(a, b) for a in (3, 2, 1) for b in (2, 1, 3, 0)] + [(0, b) for b in (2, 1, 3)]


def back_step(b):
    return (XS - b) % XS


def dot(a, b):
    return jnp.dot(a, b, preferred_element_type=F32)


def dot_t(a, b):
    return lax.dot_general(a, b, (((1,), (1,)), ((), ())), preferred_element_type=F32)


def features(u, omega_pad, kappa, lift, dim_head):
    nfeat = omega_pad[0].shape[-1]
    u32 = u.astype(F32)
    square = u32 * u32 * (-lift) - (0.5 * math.log2(nfeat) / kappa / dim_head)
    high = square.astype(BF16).astype(F32)
    low = pltpu.roll(square - high, dim_head, 1)
    first = lax.broadcasted_iota(jnp.int32, square.shape, 1) < dim_head
    out = []
    for s in range(2):
        parts = jnp.where(first, high, low) if s == 0 else jnp.where(first, low, high)
        lhs = jnp.concatenate([u, parts.astype(BF16)], axis=1)
        arg = dot(lhs, omega_pad[s])
        out.append(jnp.exp2(arg * kappa).astype(BF16))
    return out


def kernel(
    n,
    heads,
    tok_h,
    wq_h,
    wk_h,
    wv_h,
    wo_h,
    om_h,
    ck_h,
    gain_h,
    out_h,
    tok,
    wq,
    wk,
    wv,
    wo,
    om,
    ck,
    gain,
    omp,
    proj,
    vext,
    halo,
    vt,
    fq,
    pos,
    attn,
    mixed,
    outv,
    send0,
    recv0,
    send1,
    recv1,
    send2,
    recv2,
    state,
    rhs,
    in_sem,
    out_sem,
    pair_sem,
    halo_sem,
    rs_sem,
    far_sem,
    ag_sem,
    fw_sem,
):
    tokens, width = tok.shape
    cols = halo.shape[1]
    rows_here = tokens // cols
    dim_head = width // heads
    nfeat = om.shape[-1]
    pairs = heads // 2
    lanes = 2 * dim_head
    half = nfeat // 2
    kappa = dim_head ** (-0.25) * math.log2(math.e)
    lift = 0.5 * dim_head ** (-0.5) / dim_head ** (-0.25)

    me = lax.axis_index("row")
    core = me % CORES
    near = (me // CORES) % NEAR
    zl, x = near // XS, near % XS
    far_count = n // (CORES * NEAR)
    far = me // (CORES * NEAR)
    base = far * (CORES * NEAR) + core

    partner = me + 1 - 2 * core
    above, below = (me + n - 1) % n, (me + 1) % n
    near_ids = [(s, near_peer(zl, x, *s)) for s in STEPS]
    far_ids = [
        ((far + d) % far_count) * (CORES * NEAR) + near * CORES + core
        for d in range(1, far_count)
    ]

    loads = [
        pltpu.make_async_copy(src, dst, in_sem.at[i])
        for i, (src, dst) in enumerate(
            [
                (tok_h, tok),
                (wv_h, wv),
                (wk_h, wk),
                (om_h, om),
                (wq_h, wq),
                (ck_h, ck),
                (gain_h, gain),
                (wo_h, wo),
            ]
        )
    ]
    for load in loads:
        load.start()

    barrier = pltpu.get_barrier_semaphore()
    greeted = [partner, above, below] + [base + j * CORES for _, j in near_ids] + far_ids
    for other in greeted:
        pl.semaphore_signal(barrier, inc=1, device_id={"row": other}, device_id_type=MESH)

    for s in range(2):
        for p in range(pairs):
            omp[p, s, (1 - s) * dim_head : (2 - s) * dim_head, :] = jnp.zeros((dim_head, nfeat), BF16)
            omp[p, s, lanes:, :] = jnp.ones((lanes, nfeat), BF16)
    for p in range(pairs):
        vt[p, lanes:, :] = jnp.ones((vt.shape[1] - lanes, tokens), BF16)
    for h in range(2):
        for j in range(NEAR):
            send0[h, j, KV_ROWS:, :] = jnp.zeros((CHUNK - KV_ROWS, half), BF16)

    loads[0].wait()
    loads[1].wait()
    for c in range(0, width, 256):
        vext[tokens // rows_here : tokens // rows_here + tokens, c : c + 256] = dot(
            tok[...], wv[:, c : c + 256]
        ).astype(BF16)
    loads[2].wait()
    for c in range(0, width, 256):
        proj[:, c : c + 256] = dot(tok[...], wk[:, c : c + 256]).astype(BF16)
    loads[3].wait()
    for p in range(pairs):
        for s in range(2):
            omp[p, s, s * dim_head : (s + 1) * dim_head, :] = om[2 * p + s]
        vt[p, :lanes, :] = vext[cols : cols + tokens, p * lanes : (p + 1) * lanes].T

    for p in range(pairs):
        u = proj[:, p * lanes : (p + 1) * lanes]
        feats = features(u, [omp[p, 0], omp[p, 1]], kappa, lift, dim_head)
        for s in range(2):
            head = 2 * p + s
            st = dot(vt[p], feats[s])
            for h in range(2):
                part = st[:, h * half : (h + 1) * half].astype(BF16)
                for i in range(dim_head // 16):
                    block = head * (dim_head // 16) + i
                    chunk, place = divmod(block, KV_ROWS // 16)
                    send0[h, chunk, place * 16 : (place + 1) * 16, :] = part[
                        s * dim_head + i * 16 : s * dim_head + (i + 1) * 16
                    ]
                send0[h, head + head // 3, KV_ROWS:, :] = part[lanes : lanes + 16]

    pl.semaphore_wait(barrier, len(greeted))

    swap = pltpu.make_async_remote_copy(
        src_ref=send0.at[1 - core],
        dst_ref=recv0,
        send_sem=pair_sem.at[0],
        recv_sem=pair_sem.at[1],
        device_id={"row": partner},
        device_id_type=MESH,
    )
    swap.start()
    swap.wait()
    for j in range(NEAR):
        send1[j] = (send0[core, j].astype(F32) + recv0[j].astype(F32)).astype(BF16)

    near_copies = []
    for k, (step, j) in enumerate(near_ids):
        copy = pltpu.make_async_remote_copy(
            src_ref=send1.at[j],
            dst_ref=recv1.at[k],
            send_sem=rs_sem.at[0, k],
            recv_sem=rs_sem.at[1, k],
            device_id={"row": base + j * CORES},
            device_id_type=MESH,
        )
        copy.start()
        near_copies.append(copy)

    halo_copies = []
    for k, (row, other) in enumerate([(rows_here - 1, below), (0, above)]):
        copy = pltpu.make_async_remote_copy(
            src_ref=tok.at[pl.ds(row * cols, cols)],
            dst_ref=halo.at[k],
            send_sem=halo_sem.at[0, k],
            recv_sem=halo_sem.at[1, k],
            device_id={"row": other},
            device_id_type=MESH,
        )
        copy.start()
        halo_copies.append(copy)

    loads[4].wait()
    for c in range(0, width, 256):
        proj[:, c : c + 256] = dot(tok[...], wq[:, c : c + 256]).astype(BF16)
    for p in range(pairs):
        u = proj[:, p * lanes : (p + 1) * lanes]
        feats = features(u, [omp[p, 0], omp[p, 1]], kappa, lift, dim_head)
        for s in range(2):
            fq[:, (2 * p + s) * nfeat : (2 * p + s + 1) * nfeat] = feats[s]

    for copy in near_copies:
        copy.wait()
    total = send1[near].astype(F32)
    for k in range(len(STEPS)):
        total = total + recv1[k].astype(F32)
    send2[...] = total.astype(BF16)

    far_copies = []
    for k, other in enumerate(far_ids):
        copy = pltpu.make_async_remote_copy(
            src_ref=send2,
            dst_ref=recv2.at[k],
            send_sem=far_sem.at[0, k],
            recv_sem=far_sem.at[1, k],
            device_id={"row": other},
            device_id_type=MESH,
        )
        copy.start()
        far_copies.append(copy)

    for copy in halo_copies:
        copy.wait()
    for k, (edge, place) in enumerate([(0, 0), (n - 1, rows_here + 1)]):
        rows = halo[k]
        rows = jnp.where(me == edge, jnp.zeros_like(rows), rows)
        for c in range(0, width, 256):
            vext[place * cols : (place + 1) * cols, c : c + 256] = dot(rows, wv[:, c : c + 256]).astype(
                BF16
            )
    loads[5].wait()
    column = lax.broadcasted_iota(jnp.int32, (cols, lanes), 0)
    for c in range(0, width, lanes):
        for r in range(rows_here):
            rows = [
                vext[(r + a) * cols : (r + a + 1) * cols, c : c + lanes].astype(F32) for a in range(3)
            ]
            taps = []
            for b in range(3):
                tap = rows[0] * ck[b : b + 1, c : c + lanes]
                for a in (1, 2):
                    tap = tap + rows[a] * ck[3 * a + b : 3 * a + b + 1, c : c + lanes]
                taps.append(tap)
            left = jnp.where(column == 0, 0.0, pltpu.roll(taps[0], 1, 0))
            right = jnp.where(column == cols - 1, 0.0, pltpu.roll(taps[2], cols - 1, 0))
            pos[r * cols : (r + 1) * cols, c : c + lanes] = left + taps[1] + right

    for copy in far_copies:
        copy.wait()
    total = send2[...].astype(F32)
    for k in range(len(far_ids)):
        total = total + recv2[k].astype(F32)
    state[core, near] = total.astype(BF16)

    gathers = []
    for k, (step, j) in enumerate(near_ids):
        copy = pltpu.make_async_remote_copy(
            src_ref=state.at[core, near],
            dst_ref=state.at[core, near],
            send_sem=ag_sem.at[0, k],
            recv_sem=ag_sem.at[1, k],
            device_id={"row": base + j * CORES},
            device_id_type=MESH,
        )
        copy.start()
        gathers.append(copy)

    def hand_on(j, k):
        copy = pltpu.make_async_remote_copy(
            src_ref=state.at[core, j],
            dst_ref=state.at[core, j],
            send_sem=fw_sem.at[0, k],
            recv_sem=fw_sem.at[1, k],
            device_id={"row": partner},
            device_id_type=MESH,
        )
        copy.start()
        return copy

    handed = [hand_on(near, len(STEPS))]
    for k in reversed(range(len(STEPS))):
        a, b = STEPS[k]
        gathers[k].wait()
        handed.append(hand_on(near_peer(zl, x, a, back_step(b)), k))
    for copy in handed:
        copy.wait()

    blank = jnp.zeros((dim_head, half), BF16)
    for p in range(pairs):
        for h in range(2):
            parts, sums = [], []
            for s in range(2):
                head = 2 * p + s
                blocks = []
                for i in range(dim_head // 16):
                    chunk, place = divmod(head * (dim_head // 16) + i, KV_ROWS // 16)
                    blocks.append(state[h, chunk, place * 16 : (place + 1) * 16, :])
                parts.append(jnp.concatenate(blocks, axis=0))
                key_sum = state[h, head + head // 3, KV_ROWS:, :]
                sums.append(jnp.concatenate([key_sum] * (dim_head // 16), axis=0))
            for s in range(2):
                at = (2 * h + s) * half
                for i, block in enumerate([parts, sums]):
                    for t in range(2):
                        rhs[p, (2 * i + t) * dim_head : (2 * i + t + 1) * dim_head, at : at + half] = (
                            block[s] if s == t else blank
                        )

    loads[6].wait()
    loads[7].wait()
    for r in range(rows_here):
        at = slice(r * cols, (r + 1) * cols)
        squares = jnp.zeros((cols, lanes), F32)
        for p in range(pairs):
            lhs = jnp.concatenate(
                [
                    fq[at, (2 * p + s) * nfeat + h * half : (2 * p + s) * nfeat + (h + 1) * half]
                    for h in range(2)
                    for s in range(2)
                ],
                axis=1,
            )
            both = dot_t(lhs, rhs[p])
            ratio = both[:, :lanes] / both[:, lanes:]
            attn[:, p * lanes : (p + 1) * lanes] = ratio
            squares = squares + ratio * ratio
        scale = lax.rsqrt(jnp.sum(squares, axis=1, keepdims=True) * (1.0 / width) + 1e-06)
        for c in range(0, width, lanes):
            normed = attn[:, c : c + lanes] * scale * gain[:, c : c + lanes]
            mixed[:, c : c + lanes] = (normed + pos[at, c : c + lanes]).astype(BF16)
        for c in range(0, width, 256):
            outv[at, c : c + 256] = (
                tok[at, c : c + 256].astype(F32) + dot(mixed[...], wo[:, c : c + 256])
            ).astype(BF16)
        pltpu.make_async_copy(outv.at[at], out_h.at[at], out_sem.at[r]).start()
    for r in range(rows_here):
        at = slice(r * cols, (r + 1) * cols)
        pltpu.make_async_copy(outv.at[at], out_h.at[at], out_sem.at[r]).wait()


def layer(n, tokens, w_query, w_key, w_value, w_out, omega, conv_kernel, norm_gain):
    rows_here, cols, width = tokens.shape
    heads, dim_head, nfeat = omega.shape
    count = rows_here * cols
    pairs, lanes, half = heads // 2, 2 * dim_head, nfeat // 2
    far = n // (CORES * NEAR) - 1
    steps = len(STEPS)
    vmem = pltpu.VMEM
    dma = pltpu.SemaphoreType.DMA
    out = pl.pallas_call(
        functools.partial(kernel, n, heads),
        out_shape=jax.ShapeDtypeStruct((count, width), BF16),
        in_specs=[pl.BlockSpec(memory_space=pl.ANY)] * 8,
        out_specs=pl.BlockSpec(memory_space=pl.ANY),
        scratch_shapes=[
            vmem((count, width), BF16),
            vmem((width, width), BF16),
            vmem((width, width), BF16),
            vmem((width, width), BF16),
            vmem((width, width), BF16),
            vmem((heads, dim_head, nfeat), BF16),
            vmem((9, width), F32),
            vmem((1, width), F32),
            vmem((pairs, 2, 2 * lanes, nfeat), BF16),
            vmem((count, width), BF16),
            vmem((count + 2 * cols, width), BF16),
            vmem((2, cols, width), BF16),
            vmem((pairs, lanes + 16, count), BF16),
            vmem((count, heads * nfeat), BF16),
            vmem((count, width), F32),
            vmem((cols, width), F32),
            vmem((cols, width), BF16),
            vmem((count, width), BF16),
            vmem((2, NEAR, CHUNK, half), BF16),
            vmem((NEAR, CHUNK, half), BF16),
            vmem((NEAR, CHUNK, half), BF16),
            vmem((steps, CHUNK, half), BF16),
            vmem((CHUNK, half), BF16),
            vmem((far, CHUNK, half), BF16),
            vmem((2, NEAR, CHUNK, half), BF16),
            vmem((pairs, 2 * lanes, 2 * nfeat), BF16),
            dma((8,)),
            dma((rows_here,)),
            dma((2,)),
            dma((2, 2)),
            dma((2, steps)),
            dma((2, far)),
            dma((2, steps)),
            dma((2, steps + 1)),
        ],
        compiler_params=pltpu.CompilerParams(
            collective_id=0, has_side_effects=True, vmem_limit_bytes=56 * 1024 * 1024
        ),
        name="favor_layer",
    )(
        tokens.reshape(count, width),
        w_query,
        w_key,
        w_value,
        w_out,
        omega,
        conv_kernel.reshape(9, width),
        norm_gain.reshape(1, width),
    )
    return out.reshape(rows_here, cols, width)


def solution(mesh):
    return jax.shard_map(
        functools.partial(layer, mesh.shape["row"]),
        mesh=mesh,
        in_specs=(P(("parts", "row"), None, None), P(), P(), P(), P(), P(), P(), P()),
        out_specs=P(("parts", "row"), None, None),
        check_vma=False,
    )
```

time: 390 us -> 61.1 us (0.16)
  waiting for transfers between devices: 306 us -> 0 us
  Pallas kernels: 0 us -> 56.1 us
  starting transfers between devices: 24.6 us -> 0 us
  matrix products: 23 us -> 0 us
  between operations: 13.6 us -> 0.01 us
  local copies, waits for them, and re-layouts: 14.5 us -> 4.74 us
  other arithmetic: 7.49 us -> 0 us
    psum x1 -> x0, waiting for transfers between devices: 306 us -> none  [packed_total(): subtotal = lax.psum(jnp.concatenate([a.ravel() for a in arrays]), axis)]
    pallas_call x0 -> x1, Pallas kernels: none -> 56.1 us  [layer(): pl.pallas_call(functools.partial(kernel, n, heads), out_shape=jax.ShapeDt...]
    ppermute x2 -> x0, starting transfers between devices: 24.6 us -> none  [the longest x1 20 us: with_halo(): lax.ppermute(lax.slice_in_dim(block, 0, width, axis=dim), axis, backward)]
    dot_general x9 -> x0, matrix products: 23 us -> none  [the longest x2 7.39 us: feature_map(): jnp.einsum('thd,hdf->thf', heads_in, omega, preferred_element_type=jnp.fl...]
  transfers between devices with their start and end apart: 3 -> 0, of which waited for: 1 -> 0; matrix products, arithmetic and copies ran while one was open for 4% -> 0% of each run, Pallas kernels for 0% -> 0%
where the time goes in v1:
time: 61.1 us; the launch traced here: 60.8 us
  Pallas kernels  56.1 us (92%)
  local copies, waits for them, and re-layouts  4.74 us (8%)
    pallas_call x1, Pallas kernels, layer(): pl.pallas_call(functools.partial(kernel, n, heads), out_shape=jax.ShapeDt...  56.1 us
    unnamed x1, local copies, waits for them, and re-layouts  2.06 us
    reshape x1, local copies, waits for them, and re-layouts, layer(): conv_kernel.reshape(9, width)  1.4 us
    reshape x1, local copies, waits for them, and re-layouts, layer(): norm_gain.reshape(1, width)  1.28 us

profile of v1, /device:TPU:33, one launch (start us, length us, event | category | flops | bytes accessed | tf_op | source)
XLA Modules:
  0.0 60.8 jit_solution(5333188364482926922)
XLA Ops:
  0.0 1.3 %reshape.14.gain_h = f32[1,768]{1,0:T(1,128)} reshape(f32[768]{0:T(1024)} %param.15) | data formatting | bytes 6144 | tf_op jit(solution)/shard_map/reshape | solution.py:455
  1.3 1.4 %reshape.13.ck_h = f32[9,768]{1,0:T(8,128)} reshape(f32[3,3,768]{2,1,0:T(4,128)} %param.14) | data formatting | bytes 55296 | tf_op jit(solution)/shard_map/reshape | solution.py:454
  2.7 56.1 %favor_layer.1 = bf16[512,768]{1,0:T(8,128)(2,1)} custom-call(bf16[512,768]{1,0:T(8,128)(2,1)} %bitcast.3, bf16[768,768]{1,0:T(8,128)(2,1)} %wq_h.1, bf16[768,768]{1,0:T(8,128)(2,1)} %wk_h.1, bf16[768,768]{1,0:T(8,128)(2,1)} %wv_h.1, bf16[768,768]{1,0:T(8,128)(2,1)} %wo_h.1, bf16[12,64,256]{2,1,0:T(8,128)(2,1)} %om_h.1, f32[9,768]{1,0:T(8,128)} %reshape.13.ck_h, ...), custom_call_target="tpu_custom_call" | custom-call | tf_op jit(solution)/shard_map/favor_layer/pallas_call | solution.py:402
  58.8 2.1 %copy.10 = bf16[2,256,768]{2,1,0:T(8,128)(2,1)} copy(bf16[2,256,768]{2,1,0:T(8,128)(2,1)} %bitcast.2) | data formatting | bytes 1572864

commit v2 on v1

--- a/solution.py
+++ b/solution.py
@@ -17,7 +17,7 @@
 CORES = 2
 NEAR = XS * ZN
 KV_ROWS = 48
-CHUNK = 64
+CHUNK = 56
 
 
 def near_peer(zl, x, a, b):
@@ -74,7 +74,7 @@
     om_h,
     ck_h,
     gain_h,
-    out_h,
+    out,
     tok,
     wq,
     wk,
@@ -92,7 +92,6 @@
     pos,
     attn,
     mixed,
-    outv,
     send0,
     recv0,
     send1,
@@ -102,13 +101,13 @@
     state,
     rhs,
     in_sem,
-    out_sem,
     pair_sem,
     halo_sem,
     rs_sem,
     far_sem,
     ag_sem,
     fw_sem,
+    relay_sem,
 ):
     tokens, width = tok.shape
     cols = halo.shape[1]
@@ -136,29 +135,27 @@
         ((far + d) % far_count) * (CORES * NEAR) + near * CORES + core
         for d in range(1, far_count)
     ]
-
-    loads = [
-        pltpu.make_async_copy(src, dst, in_sem.at[i])
-        for i, (src, dst) in enumerate(
-            [
-                (tok_h, tok),
-                (wv_h, wv),
-                (wk_h, wk),
-                (om_h, om),
-                (wq_h, wq),
-                (ck_h, ck),
-                (gain_h, gain),
-                (wo_h, wo),
-            ]
-        )
-    ]
-    for load in loads:
-        load.start()
+    next_ids = [far_ids[0], far_ids[-1]]
 
     barrier = pltpu.get_barrier_semaphore()
-    greeted = [partner, above, below] + [base + j * CORES for _, j in near_ids] + far_ids
+    greeted = next_ids + [base + j * CORES for _, j in near_ids] + [above, below, partner]
     for other in greeted:
         pl.semaphore_signal(barrier, inc=1, device_id={"row": other}, device_id_type=MESH)
+
+    blocks = [slice(c, c + 256) for c in range(0, width, 256)]
+
+    def load(src, dst, i):
+        copy = pltpu.make_async_copy(src, dst, in_sem.at[i])
+        copy.start()
+        return copy
+
+    parts = [slice(i * width // 2, (i + 1) * width // 2) for i in range(2)]
+    tok_loads = [
+        load(tok_h.at[pl.ds(i * cols, cols)], tok.at[pl.ds(i * cols, cols)], i) for i in range(rows_here)
+    ]
+    v_loads = [load(wv_h.at[part], wv.at[part], rows_here + i) for i, part in enumerate(parts)]
+    k_loads = [load(wk_h.at[part], wk.at[part], rows_here + 2 + i) for i, part in enumerate(parts)]
+    om_load = load(om_h, om, rows_here + 4)
 
     for s in range(2):
         for p in range(pairs):
@@ -170,16 +167,20 @@
         for j in range(NEAR):
             send0[h, j, KV_ROWS:, :] = jnp.zeros((CHUNK - KV_ROWS, half), BF16)
 
-    loads[0].wait()
-    loads[1].wait()
-    for c in range(0, width, 256):
-        vext[tokens // rows_here : tokens // rows_here + tokens, c : c + 256] = dot(
-            tok[...], wv[:, c : c + 256]
-        ).astype(BF16)
-    loads[2].wait()
-    for c in range(0, width, 256):
-        proj[:, c : c + 256] = dot(tok[...], wk[:, c : c + 256]).astype(BF16)
-    loads[3].wait()
+    for copy in tok_loads + v_loads:
+        copy.wait()
+    for block in blocks:
+        vext[cols : cols + tokens, block] = dot(tok[...], wv[:, block]).astype(BF16)
+    for copy in k_loads:
+        copy.wait()
+    for block in blocks:
+        proj[:, block] = dot(tok[...], wk[:, block]).astype(BF16)
+    om_load.wait()
+    late = rows_here + 5
+    q_load = load(wq_h, wq, late)
+    ck_load = load(ck_h, ck, late + 1)
+    gain_load = load(gain_h, gain, late + 2)
+    o_load = load(wo_h, wo, late + 3)
     for p in range(pairs):
         for s in range(2):
             omp[p, s, s * dim_head : (s + 1) * dim_head, :] = om[2 * p + s]
@@ -199,9 +200,11 @@
                     send0[h, chunk, place * 16 : (place + 1) * 16, :] = part[
                         s * dim_head + i * 16 : s * dim_head + (i + 1) * 16
                     ]
-                send0[h, head + head // 3, KV_ROWS:, :] = part[lanes : lanes + 16]
+                send0[h, head + head // 3, KV_ROWS:, :] = part[lanes : lanes + CHUNK - KV_ROWS]
 
     pl.semaphore_wait(barrier, len(greeted))
+    for other in next_ids:
+        pl.semaphore_signal(relay_sem, inc=1, device_id={"row": other}, device_id_type=MESH)
 
     swap = pltpu.make_async_remote_copy(
         src_ref=send0.at[1 - core],
@@ -242,7 +245,7 @@
         copy.start()
         halo_copies.append(copy)
 
-    loads[4].wait()
+    q_load.wait()
     for c in range(0, width, 256):
         proj[:, c : c + 256] = dot(tok[...], wq[:, c : c + 256]).astype(BF16)
     for p in range(pairs):
@@ -258,8 +261,9 @@
         total = total + recv1[k].astype(F32)
     send2[...] = total.astype(BF16)
 
+    pl.semaphore_wait(relay_sem, len(next_ids))
     far_copies = []
-    for k, other in enumerate(far_ids):
+    for k, other in sorted(enumerate(far_ids), key=lambda item: abs(2 * item[0] + 2 - far_count)):
         copy = pltpu.make_async_remote_copy(
             src_ref=send2,
             dst_ref=recv2.at[k],
@@ -280,7 +284,7 @@
             vext[place * cols : (place + 1) * cols, c : c + 256] = dot(rows, wv[:, c : c + 256]).astype(
                 BF16
             )
-    loads[5].wait()
+    ck_load.wait()
     column = lax.broadcasted_iota(jnp.int32, (cols, lanes), 0)
     for c in range(0, width, lanes):
         for r in range(rows_here):
@@ -289,9 +293,9 @@
             ]
             taps = []
             for b in range(3):
-                tap = rows[0] * ck[b : b + 1, c : c + lanes]
+                tap = rows[0] * ck[0, b : b + 1, c : c + lanes]
                 for a in (1, 2):
-                    tap = tap + rows[a] * ck[3 * a + b : 3 * a + b + 1, c : c + lanes]
+                    tap = tap + rows[a] * ck[a, b : b + 1, c : c + lanes]
                 taps.append(tap)
             left = jnp.where(column == 0, 0.0, pltpu.roll(taps[0], 1, 0))
             right = jnp.where(column == cols - 1, 0.0, pltpu.roll(taps[2], cols - 1, 0))
@@ -349,7 +353,7 @@
                     blocks.append(state[h, chunk, place * 16 : (place + 1) * 16, :])
                 parts.append(jnp.concatenate(blocks, axis=0))
                 key_sum = state[h, head + head // 3, KV_ROWS:, :]
-                sums.append(jnp.concatenate([key_sum] * (dim_head // 16), axis=0))
+                sums.append(jnp.concatenate([key_sum] * (dim_head // (CHUNK - KV_ROWS)), axis=0))
             for s in range(2):
                 at = (2 * h + s) * half
                 for i, block in enumerate([parts, sums]):
@@ -358,8 +362,8 @@
                             block[s] if s == t else blank
                         )
 
-    loads[6].wait()
-    loads[7].wait()
+    gain_load.wait()
+    o_load.wait()
     for r in range(rows_here):
         at = slice(r * cols, (r + 1) * cols)
         squares = jnp.zeros((cols, lanes), F32)
@@ -374,20 +378,16 @@
             )
             both = dot_t(lhs, rhs[p])
             ratio = both[:, :lanes] / both[:, lanes:]
-            attn[:, p * lanes : (p + 1) * lanes] = ratio
+            attn[at, p * lanes : (p + 1) * lanes] = ratio
             squares = squares + ratio * ratio
         scale = lax.rsqrt(jnp.sum(squares, axis=1, keepdims=True) * (1.0 / width) + 1e-06)
         for c in range(0, width, lanes):
-            normed = attn[:, c : c + lanes] * scale * gain[:, c : c + lanes]
-            mixed[:, c : c + lanes] = (normed + pos[at, c : c + lanes]).astype(BF16)
+            normed = attn[at, c : c + lanes] * scale * gain[c : c + lanes].reshape(1, lanes)
+            mixed[at, c : c + lanes] = (normed + pos[at, c : c + lanes]).astype(BF16)
         for c in range(0, width, 256):
-            outv[at, c : c + 256] = (
-                tok[at, c : c + 256].astype(F32) + dot(mixed[...], wo[:, c : c + 256])
+            out[at, c : c + 256] = (
+                tok[at, c : c + 256].astype(F32) + dot(mixed[at], wo[:, c : c + 256])
             ).astype(BF16)
-        pltpu.make_async_copy(outv.at[at], out_h.at[at], out_sem.at[r]).start()
-    for r in range(rows_here):
-        at = slice(r * cols, (r + 1) * cols)
-        pltpu.make_async_copy(outv.at[at], out_h.at[at], out_sem.at[r]).wait()
 
 
 def layer(n, tokens, w_query, w_key, w_value, w_out, omega, conv_kernel, norm_gain):
@@ -403,7 +403,7 @@
         functools.partial(kernel, n, heads),
         out_shape=jax.ShapeDtypeStruct((count, width), BF16),
         in_specs=[pl.BlockSpec(memory_space=pl.ANY)] * 8,
-        out_specs=pl.BlockSpec(memory_space=pl.ANY),
+        out_specs=pl.BlockSpec(memory_space=pltpu.VMEM),
         scratch_shapes=[
             vmem((count, width), BF16),
             vmem((width, width), BF16),
@@ -411,8 +411,8 @@
             vmem((width, width), BF16),
             vmem((width, width), BF16),
             vmem((heads, dim_head, nfeat), BF16),
-            vmem((9, width), F32),
-            vmem((1, width), F32),
+            vmem((3, 3, width), F32),
+            vmem((width,), F32),
             vmem((pairs, 2, 2 * lanes, nfeat), BF16),
             vmem((count, width), BF16),
             vmem((count + 2 * cols, width), BF16),
@@ -420,8 +420,7 @@
             vmem((pairs, lanes + 16, count), BF16),
             vmem((count, heads * nfeat), BF16),
             vmem((count, width), F32),
-            vmem((cols, width), F32),
-            vmem((cols, width), BF16),
+            vmem((count, width), F32),
             vmem((count, width), BF16),
             vmem((2, NEAR, CHUNK, half), BF16),
             vmem((NEAR, CHUNK, half), BF16),
@@ -431,28 +430,33 @@
             vmem((far, CHUNK, half), BF16),
             vmem((2, NEAR, CHUNK, half), BF16),
             vmem((pairs, 2 * lanes, 2 * nfeat), BF16),
-            dma((8,)),
-            dma((rows_here,)),
+            dma((rows_here + 9,)),
             dma((2,)),
             dma((2, 2)),
             dma((2, steps)),
             dma((2, far)),
             dma((2, steps)),
             dma((2, steps + 1)),
+            pltpu.SemaphoreType.REGULAR,
         ],
         compiler_params=pltpu.CompilerParams(
-            collective_id=0, has_side_effects=True, vmem_limit_bytes=56 * 1024 * 1024
+            collective_id=0, has_side_effects=True, vmem_limit_bytes=48 * 1024 * 1024
         ),
         name="favor_layer",
     )(
-        tokens.reshape(count, width),
-        w_query,
-        w_key,
-        w_value,
-        w_out,
-        omega,
-        conv_kernel.reshape(9, width),
-        norm_gain.reshape(1, width),
+        *[
+            pltpu.with_memory_space_constraint(operand, pltpu.HBM)
+            for operand in (
+                tokens.reshape(count, width),
+                w_query,
+                w_key,
+                w_value,
+                w_out,
+                omega,
+                conv_kernel,
+                norm_gain,
+            )
+        ]
     )
     return out.reshape(rows_here, cols, width)
 

time: 61.1 us -> 55.8 us (0.913)
  local copies, waits for them, and re-layouts: 4.74 us -> 0.88 us
  Pallas kernels: 56.1 us -> 54.8 us
    reshape x2 -> x0, local copies, waits for them, and re-layouts: 2.68 us -> none  [the longest x1 1.4 us: layer(): conv_kernel.reshape(9, width)]
    pallas_call x1, Pallas kernels: 56.1 us -> 54.8 us  [layer(): pl.pallas_call(functools.partial(kernel, n, heads), out_shape=jax.ShapeDt...]
    unnamed x1, local copies, waits for them, and re-layouts: 2.06 us -> 0.88 us
where the time goes in v2:
time: 55.8 us; the launch traced here: 55.7 us
  Pallas kernels  54.8 us (98%)
  local copies, waits for them, and re-layouts  0.88 us (2%)
    pallas_call x1, Pallas kernels, layer(): pl.pallas_call(functools.partial(kernel, n, heads), out_shape=jax.ShapeDt...  54.8 us

profile of v2, /device:TPU:33, one launch (start us, length us, event | category | flops | bytes accessed | tf_op | source)
XLA Modules:
  0.0 55.7 jit_solution(4273548612730456359)
XLA Ops:
  0.0 54.8 %favor_layer.1 = bf16[512,768]{1,0:T(8,128)(2,1)S(1)} custom-call(bf16[512,768]{1,0:T(8,128)(2,1)} %bitcast.3, bf16[768,768]{1,0:T(8,128)(2,1)} %wq_h.1, bf16[768,768]{1,0:T(8,128)(2,1)} %wk_h.1, bf16[768,768]{1,0:T(8,128)(2,1)} %wv_h.1, bf16[768,768]{1,0:T(8,128)(2,1)} %wo_h.1, bf16[12,64,256]{2,1,0:T(8,128)(2,1)} %om_h.1, f32[3,3,768]{2,1,0:T(4,128)} %ck_h.1, ...), custom_call_target="tpu_custom_call" | custom-call | tf_op jit(solution)/shard_map/favor_layer/pallas_call | solution.py:402
  54.8 0.9 %copy.10 = bf16[2,256,768]{2,1,0:T(8,128)(2,1)} copy(bf16[2,256,768]{2,1,0:T(8,128)(2,1)S(1)} %bitcast.2) | data formatting | bytes 1572864

commit v3 on v2

--- a/solution.py
+++ b/solution.py
@@ -20,23 +20,15 @@
 CHUNK = 56
 
 
-def near_peer(zl, x, a, b):
-    if a == 0:
-        zp = zl
-    elif a == 1:
-        zp = zl + 1 - 2 * (zl % 2)
-    elif a == 2:
-        zp = (zl + 2) % 4
-    else:
-        zp = 3 - zl
-    return zp * XS + (x + b) % XS
+def slot(zl, x):
+    return (zl + x) % 2 * (NEAR // 2) + zl * (XS // 2) + x // 2
+
+
+def run_step(zl, a):
+    return [zl, zl + 1 - 2 * (zl % 2), (zl + 2) % ZN, ZN - 1 - zl][a]
 
 
 STEPS = [(a, b) for a in (3, 2, 1) for b in (2, 1, 3, 0)] + [(0, b) for b in (2, 1, 3)]
-
-
-def back_step(b):
-    return (XS - b) % XS
 
 
 def dot(a, b):
@@ -100,6 +92,7 @@
     recv2,
     state,
     rhs,
+    partial,
     in_sem,
     pair_sem,
     halo_sem,
@@ -122,25 +115,23 @@
 
     me = lax.axis_index("row")
     core = me % CORES
-    near = (me // CORES) % NEAR
-    zl, x = near // XS, near % XS
-    far_count = n // (CORES * NEAR)
-    far = me // (CORES * NEAR)
-    base = far * (CORES * NEAR) + core
+    x = (me // CORES) % XS
+    z_count = n // (CORES * XS)
+    far_count = z_count // ZN
+    shift = core * (ZN // 2)
+    z = (me // (CORES * XS) + shift) % z_count
+    zl, far = z % ZN, z // ZN
+    near = slot(zl, x)
+
+    def device(run, zl, x):
+        return (((run * ZN + zl + z_count - shift) % z_count) * XS + x) * CORES + core
 
     partner = me + 1 - 2 * core
     above, below = (me + n - 1) % n, (me + 1) % n
-    near_ids = [(s, near_peer(zl, x, *s)) for s in STEPS]
-    far_ids = [
-        ((far + d) % far_count) * (CORES * NEAR) + near * CORES + core
-        for d in range(1, far_count)
-    ]
+    near_to = [(run_step(zl, a), (x + b) % XS) for a, b in STEPS]
+    near_from = [(run_step(zl, a), (x + XS - b) % XS) for a, b in STEPS]
+    far_ids = [device((far + d) % far_count, zl, x) for d in range(1, far_count)]
     next_ids = [far_ids[0], far_ids[-1]]
-
-    barrier = pltpu.get_barrier_semaphore()
-    greeted = next_ids + [base + j * CORES for _, j in near_ids] + [above, below, partner]
-    for other in greeted:
-        pl.semaphore_signal(barrier, inc=1, device_id={"row": other}, device_id_type=MESH)
 
     blocks = [slice(c, c + 256) for c in range(0, width, 256)]
 
@@ -156,6 +147,11 @@
     v_loads = [load(wv_h.at[part], wv.at[part], rows_here + i) for i, part in enumerate(parts)]
     k_loads = [load(wk_h.at[part], wk.at[part], rows_here + 2 + i) for i, part in enumerate(parts)]
     om_load = load(om_h, om, rows_here + 4)
+
+    barrier = pltpu.get_barrier_semaphore()
+    greeted = next_ids + [device(far, *to) for to in near_to] + [above, below, partner]
+    for other in greeted:
+        pl.semaphore_signal(barrier, inc=1, device_id={"row": other}, device_id_type=MESH)
 
     for s in range(2):
         for p in range(pairs):
@@ -186,64 +182,71 @@
             omp[p, s, s * dim_head : (s + 1) * dim_head, :] = om[2 * p + s]
         vt[p, :lanes, :] = vext[cols : cols + tokens, p * lanes : (p + 1) * lanes].T
 
-    for p in range(pairs):
-        u = proj[:, p * lanes : (p + 1) * lanes]
-        feats = features(u, [omp[p, 0], omp[p, 1]], kappa, lift, dim_head)
-        for s in range(2):
-            head = 2 * p + s
-            st = dot(vt[p], feats[s])
-            for h in range(2):
-                part = st[:, h * half : (h + 1) * half].astype(BF16)
-                for i in range(dim_head // 16):
-                    block = head * (dim_head // 16) + i
-                    chunk, place = divmod(block, KV_ROWS // 16)
-                    send0[h, chunk, place * 16 : (place + 1) * 16, :] = part[
-                        s * dim_head + i * 16 : s * dim_head + (i + 1) * 16
-                    ]
-                send0[h, head + head // 3, KV_ROWS:, :] = part[lanes : lanes + CHUNK - KV_ROWS]
-
+    def local(own_pairs):
+        for p in own_pairs:
+            u = proj[:, p * lanes : (p + 1) * lanes]
+            feats = features(u, [omp[p, 0], omp[p, 1]], kappa, lift, dim_head)
+            for s in range(2):
+                head = 2 * p + s
+                st = dot(vt[p], feats[s])
+                for h in range(2):
+                    part = st[:, h * half : (h + 1) * half].astype(BF16)
+                    for i in range(dim_head // 16):
+                        block = head * (dim_head // 16) + i
+                        chunk, place = divmod(block, KV_ROWS // 16)
+                        send0[h, chunk, place * 16 : (place + 1) * 16, :] = part[
+                            s * dim_head + i * 16 : s * dim_head + (i + 1) * 16
+                        ]
+                    send0[h, head + head // 3, KV_ROWS:, :] = part[lanes : lanes + CHUNK - KV_ROWS]
+
+    def swap(wave):
+        own = pl.ds(wave * NEAR // 2, NEAR // 2)
+        copy = pltpu.make_async_remote_copy(
+            src_ref=send0.at[1 - core, own],
+            dst_ref=recv0.at[own],
+            send_sem=pair_sem.at[0, wave],
+            recv_sem=pair_sem.at[1, wave],
+            device_id={"row": partner},
+            device_id_type=MESH,
+        )
+        copy.start()
+        return copy
+
+    def scatter_copy(to, source, place):
+        return pltpu.make_async_remote_copy(
+            src_ref=send1.at[slot(*to)],
+            dst_ref=recv1.at[place],
+            send_sem=rs_sem.at[0, slot(*to)],
+            recv_sem=rs_sem.at[1, source],
+            device_id={"row": device(far, *to)},
+            device_id_type=MESH,
+        )
+
+    def scatter(wave):
+        for a in (3, 2, 1, 0):
+            zp = run_step(zl, a)
+            odd = (wave + zp + x) % 2
+            for b in (2, 0):
+                to = (zp, (x + odd + b) % XS)
+                j = slot(*to)
+                send1[j] = (send0[core, j].astype(F32) + recv0[j].astype(F32)).astype(BF16)
+                copy = scatter_copy(to, near, near)
+                if a == 0 and b == 0:
+                    pl.when(odd == 1)(copy.start)
+                else:
+                    copy.start()
+
+    local(range(pairs // 2))
     pl.semaphore_wait(barrier, len(greeted))
     for other in next_ids:
         pl.semaphore_signal(relay_sem, inc=1, device_id={"row": other}, device_id_type=MESH)
-
-    swap = pltpu.make_async_remote_copy(
-        src_ref=send0.at[1 - core],
-        dst_ref=recv0,
-        send_sem=pair_sem.at[0],
-        recv_sem=pair_sem.at[1],
-        device_id={"row": partner},
-        device_id_type=MESH,
-    )
-    swap.start()
-    swap.wait()
-    for j in range(NEAR):
-        send1[j] = (send0[core, j].astype(F32) + recv0[j].astype(F32)).astype(BF16)
-
-    near_copies = []
-    for k, (step, j) in enumerate(near_ids):
-        copy = pltpu.make_async_remote_copy(
-            src_ref=send1.at[j],
-            dst_ref=recv1.at[k],
-            send_sem=rs_sem.at[0, k],
-            recv_sem=rs_sem.at[1, k],
-            device_id={"row": base + j * CORES},
-            device_id_type=MESH,
-        )
-        copy.start()
-        near_copies.append(copy)
-
-    halo_copies = []
-    for k, (row, other) in enumerate([(rows_here - 1, below), (0, above)]):
-        copy = pltpu.make_async_remote_copy(
-            src_ref=tok.at[pl.ds(row * cols, cols)],
-            dst_ref=halo.at[k],
-            send_sem=halo_sem.at[0, k],
-            recv_sem=halo_sem.at[1, k],
-            device_id={"row": other},
-            device_id_type=MESH,
-        )
-        copy.start()
-        halo_copies.append(copy)
+    first = swap(0)
+    local(range(pairs // 2, pairs))
+    second = swap(1)
+    first.wait()
+    scatter(0)
+    second.wait()
+    scatter(1)
 
     q_load.wait()
     for c in range(0, width, 256):
@@ -252,12 +255,14 @@
         u = proj[:, p * lanes : (p + 1) * lanes]
         feats = features(u, [omp[p, 0], omp[p, 1]], kappa, lift, dim_head)
         for s in range(2):
-            fq[:, (2 * p + s) * nfeat : (2 * p + s + 1) * nfeat] = feats[s]
-
-    for copy in near_copies:
-        copy.wait()
-    total = send1[near].astype(F32)
-    for k in range(len(STEPS)):
+            for h in range(2):
+                fq[h, :, (2 * p + s) * half : (2 * p + s + 1) * half] = feats[s][:, h * half : (h + 1) * half]
+
+    for to, source in zip(near_to, near_from):
+        scatter_copy(to, slot(*source), slot(*source)).wait()
+    recv1[near] = send1[near]
+    total = recv1[0].astype(F32)
+    for k in range(1, NEAR):
         total = total + recv1[k].astype(F32)
     send2[...] = total.astype(BF16)
 
@@ -274,6 +279,39 @@
         )
         copy.start()
         far_copies.append(copy)
+
+    halo_copies = []
+    for k, (row, other) in enumerate([(rows_here - 1, below), (0, above)]):
+        copy = pltpu.make_async_remote_copy(
+            src_ref=tok.at[pl.ds(row * cols, cols)],
+            dst_ref=halo.at[k],
+            send_sem=halo_sem.at[0, k],
+            recv_sem=halo_sem.at[1, k],
+            device_id={"row": other},
+            device_id_type=MESH,
+        )
+        copy.start()
+        halo_copies.append(copy)
+
+    for copy in far_copies:
+        copy.wait()
+    total = send2[...].astype(F32)
+    for k in range(len(far_ids)):
+        total = total + recv2[k].astype(F32)
+    state[core, near] = total.astype(BF16)
+
+    gathers = []
+    for k, to in enumerate(near_to):
+        copy = pltpu.make_async_remote_copy(
+            src_ref=state.at[core, near],
+            dst_ref=state.at[core, near],
+            send_sem=ag_sem.at[0, k],
+            recv_sem=ag_sem.at[1, k],
+            device_id={"row": device(far, *to)},
+            device_id_type=MESH,
+        )
+        copy.start()
+        gathers.append(copy)
 
     for copy in halo_copies:
         copy.wait()
@@ -301,26 +339,6 @@
             right = jnp.where(column == cols - 1, 0.0, pltpu.roll(taps[2], cols - 1, 0))
             pos[r * cols : (r + 1) * cols, c : c + lanes] = left + taps[1] + right
 
-    for copy in far_copies:
-        copy.wait()
-    total = send2[...].astype(F32)
-    for k in range(len(far_ids)):
-        total = total + recv2[k].astype(F32)
-    state[core, near] = total.astype(BF16)
-
-    gathers = []
-    for k, (step, j) in enumerate(near_ids):
-        copy = pltpu.make_async_remote_copy(
-            src_ref=state.at[core, near],
-            dst_ref=state.at[core, near],
-            send_sem=ag_sem.at[0, k],
-            recv_sem=ag_sem.at[1, k],
-            device_id={"row": base + j * CORES},
-            device_id_type=MESH,
-        )
-        copy.start()
-        gathers.append(copy)
-
     def hand_on(j, k):
         copy = pltpu.make_async_remote_copy(
             src_ref=state.at[core, j],
@@ -335,48 +353,44 @@
 
     handed = [hand_on(near, len(STEPS))]
     for k in reversed(range(len(STEPS))):
-        a, b = STEPS[k]
         gathers[k].wait()
-        handed.append(hand_on(near_peer(zl, x, a, back_step(b)), k))
-    for copy in handed:
-        copy.wait()
-
+        handed.append(hand_on(slot(*near_from[k]), k))
     blank = jnp.zeros((dim_head, half), BF16)
-    for p in range(pairs):
-        for h in range(2):
+
+    def operand(slot, h):
+        for p in range(pairs):
             parts, sums = [], []
             for s in range(2):
                 head = 2 * p + s
-                blocks = []
+                tiles = []
                 for i in range(dim_head // 16):
                     chunk, place = divmod(head * (dim_head // 16) + i, KV_ROWS // 16)
-                    blocks.append(state[h, chunk, place * 16 : (place + 1) * 16, :])
-                parts.append(jnp.concatenate(blocks, axis=0))
+                    tiles.append(state[h, chunk, place * 16 : (place + 1) * 16, :])
+                parts.append(jnp.concatenate(tiles, axis=0))
                 key_sum = state[h, head + head // 3, KV_ROWS:, :]
                 sums.append(jnp.concatenate([key_sum] * (dim_head // (CHUNK - KV_ROWS)), axis=0))
             for s in range(2):
-                at = (2 * h + s) * half
                 for i, block in enumerate([parts, sums]):
                     for t in range(2):
-                        rhs[p, (2 * i + t) * dim_head : (2 * i + t + 1) * dim_head, at : at + half] = (
+                        rhs[slot, p, (2 * i + t) * dim_head : (2 * i + t + 1) * dim_head, s * half : (s + 1) * half] = (
                             block[s] if s == t else blank
                         )
 
+    operand(0, core)
+    for p in range(pairs):
+        at = slice(p * 2 * lanes, (p + 1) * 2 * lanes)
+        partial[:, at] = dot_t(fq[core, :, at], rhs[0, p])
+    for copy in handed:
+        copy.wait()
+    operand(1, 1 - core)
     gain_load.wait()
     o_load.wait()
     for r in range(rows_here):
         at = slice(r * cols, (r + 1) * cols)
         squares = jnp.zeros((cols, lanes), F32)
         for p in range(pairs):
-            lhs = jnp.concatenate(
-                [
-                    fq[at, (2 * p + s) * nfeat + h * half : (2 * p + s) * nfeat + (h + 1) * half]
-                    for h in range(2)
-                    for s in range(2)
-                ],
-                axis=1,
-            )
-            both = dot_t(lhs, rhs[p])
+            on = slice(p * 2 * lanes, (p + 1) * 2 * lanes)
+            both = partial[at, on] + dot_t(fq[1 - core, at, on], rhs[1, p])
             ratio = both[:, :lanes] / both[:, lanes:]
             attn[at, p * lanes : (p + 1) * lanes] = ratio
             squares = squares + ratio * ratio
@@ -418,22 +432,23 @@
             vmem((count + 2 * cols, width), BF16),
             vmem((2, cols, width), BF16),
             vmem((pairs, lanes + 16, count), BF16),
-            vmem((count, heads * nfeat), BF16),
+            vmem((2, count, heads * half), BF16),
             vmem((count, width), F32),
             vmem((count, width), F32),
             vmem((count, width), BF16),
             vmem((2, NEAR, CHUNK, half), BF16),
             vmem((NEAR, CHUNK, half), BF16),
             vmem((NEAR, CHUNK, half), BF16),
-            vmem((steps, CHUNK, half), BF16),
+            vmem((NEAR, CHUNK, half), BF16),
             vmem((CHUNK, half), BF16),
             vmem((far, CHUNK, half), BF16),
             vmem((2, NEAR, CHUNK, half), BF16),
-            vmem((pairs, 2 * lanes, 2 * nfeat), BF16),
+            vmem((2, pairs, 2 * lanes, nfeat), BF16),
+            vmem((count, pairs * 2 * lanes), F32),
             dma((rows_here + 9,)),
-            dma((2,)),
             dma((2, 2)),
-            dma((2, steps)),
+            dma((2, 2)),
+            dma((2, NEAR)),
             dma((2, far)),
             dma((2, steps)),
             dma((2, steps + 1)),

time: 55.8 us -> 52.4 us (0.939)
  Pallas kernels: 54.8 us -> 51.4 us
    pallas_call x1, Pallas kernels: 54.8 us -> 51.4 us  [layer(): pl.pallas_call(functools.partial(kernel, n, heads), out_shape=jax.ShapeDt...]
where the time goes in v3:
time: 52.4 us; the launch traced here: 52.3 us
  Pallas kernels  51.4 us (98%)
  local copies, waits for them, and re-layouts  0.88 us (2%)
    pallas_call x1, Pallas kernels, layer(): pl.pallas_call(functools.partial(kernel, n, heads), out_shape=jax.ShapeDt...  51.4 us

profile of v3, /device:TPU:33, one launch (start us, length us, event | category | flops | bytes accessed | tf_op | source)
XLA Modules:
  0.0 52.3 jit_solution(2762789986841222822)
XLA Ops:
  0.0 51.4 %favor_layer.1 = bf16[512,768]{1,0:T(8,128)(2,1)S(1)} custom-call(bf16[512,768]{1,0:T(8,128)(2,1)} %bitcast.3, bf16[768,768]{1,0:T(8,128)(2,1)} %wq_h.1, bf16[768,768]{1,0:T(8,128)(2,1)} %wk_h.1, bf16[768,768]{1,0:T(8,128)(2,1)} %wv_h.1, bf16[768,768]{1,0:T(8,128)(2,1)} %wo_h.1, bf16[12,64,256]{2,1,0:T(8,128)(2,1)} %om_h.1, f32[3,3,768]{2,1,0:T(4,128)} %ck_h.1, ...), custom_call_target="tpu_custom_call" | custom-call | tf_op jit(solution)/shard_map/favor_layer/pallas_call | solution.py:416
  51.4 0.9 %copy.10 = bf16[2,256,768]{2,1,0:T(8,128)(2,1)} copy(bf16[2,256,768]{2,1,0:T(8,128)(2,1)S(1)} %bitcast.2) | data formatting | bytes 1572864

commit v4 on v3

--- a/solution.py
+++ b/solution.py
@@ -16,12 +16,13 @@
 ZN = 4
 CORES = 2
 NEAR = XS * ZN
+WAVES = XS
 KV_ROWS = 48
 CHUNK = 56
 
 
 def slot(zl, x):
-    return (zl + x) % 2 * (NEAR // 2) + zl * (XS // 2) + x // 2
+    return (zl + x) % WAVES * ZN + zl
 
 
 def run_step(zl, a):
@@ -140,13 +141,10 @@
         copy.start()
         return copy
 
-    parts = [slice(i * width // 2, (i + 1) * width // 2) for i in range(2)]
-    tok_loads = [
-        load(tok_h.at[pl.ds(i * cols, cols)], tok.at[pl.ds(i * cols, cols)], i) for i in range(rows_here)
-    ]
-    v_loads = [load(wv_h.at[part], wv.at[part], rows_here + i) for i, part in enumerate(parts)]
-    k_loads = [load(wk_h.at[part], wk.at[part], rows_here + 2 + i) for i, part in enumerate(parts)]
-    om_load = load(om_h, om, rows_here + 4)
+    tok_load = load(tok_h, tok, 0)
+    v_load = load(wv_h, wv, 1)
+    k_load = load(wk_h, wk, 2)
+    om_load = load(om_h, om, 3)
 
     barrier = pltpu.get_barrier_semaphore()
     greeted = next_ids + [device(far, *to) for to in near_to] + [above, below, partner]
@@ -163,20 +161,18 @@
         for j in range(NEAR):
             send0[h, j, KV_ROWS:, :] = jnp.zeros((CHUNK - KV_ROWS, half), BF16)
 
-    for copy in tok_loads + v_loads:
-        copy.wait()
+    tok_load.wait()
+    v_load.wait()
     for block in blocks:
         vext[cols : cols + tokens, block] = dot(tok[...], wv[:, block]).astype(BF16)
-    for copy in k_loads:
-        copy.wait()
+    k_load.wait()
     for block in blocks:
         proj[:, block] = dot(tok[...], wk[:, block]).astype(BF16)
     om_load.wait()
-    late = rows_here + 5
-    q_load = load(wq_h, wq, late)
-    ck_load = load(ck_h, ck, late + 1)
-    gain_load = load(gain_h, gain, late + 2)
-    o_load = load(wo_h, wo, late + 3)
+    q_load = load(wq_h, wq, 4)
+    ck_load = load(ck_h, ck, 5)
+    gain_load = load(gain_h, gain, 6)
+    o_load = load(wo_h, wo, 7)
     for p in range(pairs):
         for s in range(2):
             omp[p, s, s * dim_head : (s + 1) * dim_head, :] = om[2 * p + s]
@@ -199,54 +195,69 @@
                         ]
                     send0[h, head + head // 3, KV_ROWS:, :] = part[lanes : lanes + CHUNK - KV_ROWS]
 
-    def swap(wave):
-        own = pl.ds(wave * NEAR // 2, NEAR // 2)
+    def send(src, dst, sems, recv, other):
         copy = pltpu.make_async_remote_copy(
-            src_ref=send0.at[1 - core, own],
-            dst_ref=recv0.at[own],
-            send_sem=pair_sem.at[0, wave],
-            recv_sem=pair_sem.at[1, wave],
-            device_id={"row": partner},
+            src_ref=src,
+            dst_ref=dst,
+            send_sem=sems.at[0],
+            recv_sem=sems.at[recv],
+            device_id={"row": other},
             device_id_type=MESH,
         )
         copy.start()
-        return copy
-
-    def scatter_copy(to, source, place):
-        return pltpu.make_async_remote_copy(
-            src_ref=send1.at[slot(*to)],
-            dst_ref=recv1.at[place],
-            send_sem=rs_sem.at[0, slot(*to)],
-            recv_sem=rs_sem.at[1, source],
-            device_id={"row": device(far, *to)},
+
+    def wait_sent(ref, sems):
+        pltpu.make_async_remote_copy(
+            src_ref=ref,
+            dst_ref=ref,
+            send_sem=sems.at[0],
+            recv_sem=sems.at[1],
+            device_id={"row": partner},
             device_id_type=MESH,
-        )
+        ).wait_send()
+
+    def wait_received(ref, sems, recv=1):
+        pltpu.make_async_remote_copy(
+            src_ref=ref,
+            dst_ref=ref,
+            send_sem=sems.at[0],
+            recv_sem=sems.at[recv],
+            device_id={"row": partner},
+            device_id_type=MESH,
+        ).wait_recv()
+
+    def swap(wave):
+        own = pl.ds(wave * ZN, ZN)
+        send(send0.at[1 - core, own], recv0.at[own], pair_sem, 1 + wave, partner)
 
     def scatter(wave):
         for a in (3, 2, 1, 0):
             zp = run_step(zl, a)
-            odd = (wave + zp + x) % 2
-            for b in (2, 0):
-                to = (zp, (x + odd + b) % XS)
-                j = slot(*to)
-                send1[j] = (send0[core, j].astype(F32) + recv0[j].astype(F32)).astype(BF16)
-                copy = scatter_copy(to, near, near)
-                if a == 0 and b == 0:
-                    pl.when(odd == 1)(copy.start)
-                else:
-                    copy.start()
-
-    local(range(pairs // 2))
+            to = (zp, (wave + WAVES - zp) % XS)
+            j = slot(*to)
+            send1[j] = (send0[core, j].astype(F32) + recv0[j].astype(F32)).astype(BF16)
+            start = functools.partial(send, send1.at[j], recv1.at[near], rs_sem, 1, device(far, *to))
+            if a == 0:
+                pl.when(to[1] != x)(start)
+            else:
+                start()
+
+    local([0, 1])
     pl.semaphore_wait(barrier, len(greeted))
     for other in next_ids:
         pl.semaphore_signal(relay_sem, inc=1, device_id={"row": other}, device_id_type=MESH)
-    first = swap(0)
-    local(range(pairs // 2, pairs))
-    second = swap(1)
-    first.wait()
+    swap(0)
+    local([2])
+    swap(1)
+    local([3, 4])
+    swap(2)
+    wait_received(recv0.at[pl.ds(0, ZN)], pair_sem, 1)
     scatter(0)
-    second.wait()
-    scatter(1)
+    local(range(5, pairs))
+    swap(3)
+    for wave in range(1, WAVES):
+        wait_received(recv0.at[pl.ds(wave * ZN, ZN)], pair_sem, 1 + wave)
+        scatter(wave)
 
     q_load.wait()
     for c in range(0, width, 256):
@@ -258,8 +269,7 @@
             for h in range(2):
                 fq[h, :, (2 * p + s) * half : (2 * p + s + 1) * half] = feats[s][:, h * half : (h + 1) * half]
 
-    for to, source in zip(near_to, near_from):
-        scatter_copy(to, slot(*source), slot(*source)).wait()
+    wait_received(recv1.at[pl.ds(0, NEAR - 1)], rs_sem)
     recv1[near] = send1[near]
     total = recv1[0].astype(F32)
     for k in range(1, NEAR):
@@ -267,54 +277,22 @@
     send2[...] = total.astype(BF16)
 
     pl.semaphore_wait(relay_sem, len(next_ids))
-    far_copies = []
     for k, other in sorted(enumerate(far_ids), key=lambda item: abs(2 * item[0] + 2 - far_count)):
-        copy = pltpu.make_async_remote_copy(
-            src_ref=send2,
-            dst_ref=recv2.at[k],
-            send_sem=far_sem.at[0, k],
-            recv_sem=far_sem.at[1, k],
-            device_id={"row": other},
-            device_id_type=MESH,
-        )
-        copy.start()
-        far_copies.append(copy)
-
-    halo_copies = []
+        send(send2, recv2.at[k], far_sem, 1, other)
+
     for k, (row, other) in enumerate([(rows_here - 1, below), (0, above)]):
-        copy = pltpu.make_async_remote_copy(
-            src_ref=tok.at[pl.ds(row * cols, cols)],
-            dst_ref=halo.at[k],
-            send_sem=halo_sem.at[0, k],
-            recv_sem=halo_sem.at[1, k],
-            device_id={"row": other},
-            device_id_type=MESH,
-        )
-        copy.start()
-        halo_copies.append(copy)
-
-    for copy in far_copies:
-        copy.wait()
+        send(tok.at[pl.ds(row * cols, cols)], halo.at[k], halo_sem, 1, other)
+
+    wait_received(recv2, far_sem)
     total = send2[...].astype(F32)
     for k in range(len(far_ids)):
         total = total + recv2[k].astype(F32)
     state[core, near] = total.astype(BF16)
 
-    gathers = []
-    for k, to in enumerate(near_to):
-        copy = pltpu.make_async_remote_copy(
-            src_ref=state.at[core, near],
-            dst_ref=state.at[core, near],
-            send_sem=ag_sem.at[0, k],
-            recv_sem=ag_sem.at[1, k],
-            device_id={"row": device(far, *to)},
-            device_id_type=MESH,
-        )
-        copy.start()
-        gathers.append(copy)
-
-    for copy in halo_copies:
-        copy.wait()
+    for (a, b), to in zip(STEPS, near_to):
+        send(state.at[core, near], state.at[core, near], ag_sem, 1 + a, device(far, *to))
+
+    wait_received(halo, halo_sem)
     for k, (edge, place) in enumerate([(0, 0), (n - 1, rows_here + 1)]):
         rows = halo[k]
         rows = jnp.where(me == edge, jnp.zeros_like(rows), rows)
@@ -339,22 +317,16 @@
             right = jnp.where(column == cols - 1, 0.0, pltpu.roll(taps[2], cols - 1, 0))
             pos[r * cols : (r + 1) * cols, c : c + lanes] = left + taps[1] + right
 
-    def hand_on(j, k):
-        copy = pltpu.make_async_remote_copy(
-            src_ref=state.at[core, j],
-            dst_ref=state.at[core, j],
-            send_sem=fw_sem.at[0, k],
-            recv_sem=fw_sem.at[1, k],
-            device_id={"row": partner},
-            device_id_type=MESH,
-        )
-        copy.start()
-        return copy
-
-    handed = [hand_on(near, len(STEPS))]
-    for k in reversed(range(len(STEPS))):
-        gathers[k].wait()
-        handed.append(hand_on(slot(*near_from[k]), k))
+    def hand_on(j):
+        send(state.at[core, j], state.at[core, j], fw_sem, 1, partner)
+
+    hand_on(near)
+    for a in range(ZN):
+        sources = [source for (step, b), source in zip(STEPS, near_from) if step == a]
+        wait_received(state.at[core, pl.ds(0, len(sources))], ag_sem, 1 + a)
+        for source in sources:
+            hand_on(slot(*source))
+
     blank = jnp.zeros((dim_head, half), BF16)
 
     def operand(slot, h):
@@ -380,19 +352,25 @@
     for p in range(pairs):
         at = slice(p * 2 * lanes, (p + 1) * 2 * lanes)
         partial[:, at] = dot_t(fq[core, :, at], rhs[0, p])
-    for copy in handed:
-        copy.wait()
+    wait_received(state.at[1 - core], fw_sem)
+    wait_sent(send0.at[1 - core], pair_sem)
+    wait_sent(send1.at[pl.ds(0, NEAR - 1)], rs_sem)
+    wait_sent(recv2, far_sem)
+    wait_sent(halo, halo_sem)
+    wait_sent(state.at[core, pl.ds(0, NEAR - 1)], ag_sem)
+    wait_sent(state.at[core], fw_sem)
     operand(1, 1 - core)
     gain_load.wait()
     o_load.wait()
+    for p in range(pairs):
+        on = slice(p * 2 * lanes, (p + 1) * 2 * lanes)
+        both = partial[:, on] + dot_t(fq[1 - core, :, on], rhs[1, p])
+        attn[:, p * lanes : (p + 1) * lanes] = both[:, :lanes] / both[:, lanes:]
     for r in range(rows_here):
         at = slice(r * cols, (r + 1) * cols)
         squares = jnp.zeros((cols, lanes), F32)
-        for p in range(pairs):
-            on = slice(p * 2 * lanes, (p + 1) * 2 * lanes)
-            both = partial[at, on] + dot_t(fq[1 - core, at, on], rhs[1, p])
-            ratio = both[:, :lanes] / both[:, lanes:]
-            attn[at, p * lanes : (p + 1) * lanes] = ratio
+        for c in range(0, width, lanes):
+            ratio = attn[at, c : c + lanes]
             squares = squares + ratio * ratio
         scale = lax.rsqrt(jnp.sum(squares, axis=1, keepdims=True) * (1.0 / width) + 1e-06)
         for c in range(0, width, lanes):
@@ -445,13 +423,13 @@
             vmem((2, NEAR, CHUNK, half), BF16),
             vmem((2, pairs, 2 * lanes, nfeat), BF16),
             vmem((count, pairs * 2 * lanes), F32),
-            dma((rows_here + 9,)),
-            dma((2, 2)),
-            dma((2, 2)),
-            dma((2, NEAR)),
-            dma((2, far)),
-            dma((2, steps)),
-            dma((2, steps + 1)),
+            dma((8,)),
+            dma((1 + WAVES,)),
+            dma((2,)),
+            dma((2,)),
+            dma((2,)),
+            dma((1 + ZN,)),
+            dma((2,)),
             pltpu.SemaphoreType.REGULAR,
         ],
         compiler_params=pltpu.CompilerParams(

time: 52.4 us -> 51.2 us (0.977)
  Pallas kernels: 51.4 us -> 50.3 us
    pallas_call x1, Pallas kernels: 51.4 us -> 50.3 us  [layer(): pl.pallas_call(functools.partial(kernel, n, heads), out_shape=jax.ShapeDt...]
where the time goes in v4:
time: 51.2 us; the launch traced here: 51.1 us
  Pallas kernels  50.3 us (98%)
  local copies, waits for them, and re-layouts  0.88 us (2%)
    pallas_call x1, Pallas kernels, layer(): pl.pallas_call(functools.partial(kernel, n, heads), out_shape=jax.ShapeDt...  50.3 us

profile of v4, /device:TPU:33, one launch (start us, length us, event | category | flops | bytes accessed | tf_op | source)
XLA Modules:
  0.0 51.1 jit_solution(10274870290822142294)
XLA Ops:
  0.0 50.3 %favor_layer.1 = bf16[512,768]{1,0:T(8,128)(2,1)S(1)} custom-call(bf16[512,768]{1,0:T(8,128)(2,1)} %bitcast.3, bf16[768,768]{1,0:T(8,128)(2,1)} %wq_h.1, bf16[768,768]{1,0:T(8,128)(2,1)} %wk_h.1, bf16[768,768]{1,0:T(8,128)(2,1)} %wv_h.1, bf16[768,768]{1,0:T(8,128)(2,1)} %wo_h.1, bf16[12,64,256]{2,1,0:T(8,128)(2,1)} %om_h.1, f32[3,3,768]{2,1,0:T(4,128)} %ck_h.1, ...), custom_call_target="tpu_custom_call" | custom-call | tf_op jit(solution)/shard_map/favor_layer/pallas_call | solution.py:394
  50.3 0.9 %copy.10 = bf16[2,256,768]{2,1,0:T(8,128)(2,1)} copy(bf16[2,256,768]{2,1,0:T(8,128)(2,1)S(1)} %bitcast.2) | data formatting | bytes 1572864

commit v5 on v4

--- a/solution.py
+++ b/solution.py
@@ -114,6 +114,18 @@
     kappa = dim_head ** (-0.25) * math.log2(math.e)
     lift = 0.5 * dim_head ** (-0.5) / dim_head ** (-0.25)
 
+    blocks = [slice(c, c + 256) for c in range(0, width, 256)]
+
+    def load(src, dst, i):
+        copy = pltpu.make_async_copy(src, dst, in_sem.at[i])
+        copy.start()
+        return copy
+
+    tok_load = load(tok_h, tok, 0)
+    v_load = load(wv_h, wv, 1)
+    k_load = load(wk_h, wk, 2)
+    om_load = load(om_h, om, 3)
+
     me = lax.axis_index("row")
     core = me % CORES
     x = (me // CORES) % XS
@@ -134,20 +146,17 @@
     far_ids = [device((far + d) % far_count, zl, x) for d in range(1, far_count)]
     next_ids = [far_ids[0], far_ids[-1]]
 
-    blocks = [slice(c, c + 256) for c in range(0, width, 256)]
-
-    def load(src, dst, i):
-        copy = pltpu.make_async_copy(src, dst, in_sem.at[i])
-        copy.start()
-        return copy
-
-    tok_load = load(tok_h, tok, 0)
-    v_load = load(wv_h, wv, 1)
-    k_load = load(wk_h, wk, 2)
-    om_load = load(om_h, om, 3)
-
     barrier = pltpu.get_barrier_semaphore()
-    greeted = next_ids + [device(far, *to) for to in near_to] + [above, below, partner]
+    greeted = [device(far, *to) for to in near_to] + [above, below, partner]
+
+    def tell_runs(sem):
+        for end, other in zip((far_count - 2, far_count - 1), next_ids):
+
+            @pl.when(far != end)
+            def _(other=other):
+                pl.semaphore_signal(sem, inc=1, device_id={"row": other}, device_id_type=MESH)
+
+    tell_runs(barrier)
     for other in greeted:
         pl.semaphore_signal(barrier, inc=1, device_id={"row": other}, device_id_type=MESH)
 
@@ -243,9 +252,8 @@
                 start()
 
     local([0, 1])
-    pl.semaphore_wait(barrier, len(greeted))
-    for other in next_ids:
-        pl.semaphore_signal(relay_sem, inc=1, device_id={"row": other}, device_id_type=MESH)
+    pl.semaphore_wait(barrier, len(greeted) + 2 - far // (far_count // 2))
+    tell_runs(relay_sem)
     swap(0)
     local([2])
     swap(1)
@@ -269,6 +277,23 @@
             for h in range(2):
                 fq[h, :, (2 * p + s) * half : (2 * p + s + 1) * half] = feats[s][:, h * half : (h + 1) * half]
 
+    line = CORES * XS
+
+    def halo_rows(crossing):
+        for k, (row, other, end) in enumerate([(rows_here - 1, below, line - 1), (0, above, 0)]):
+            start = functools.partial(
+                send, tok.at[pl.ds(row * cols, cols)], halo.at[k], halo_sem, 1, other
+            )
+            pl.when(me % line == end if crossing else me % line != end)(start)
+
+    halo_rows(False)
+
+    @pl.when(far < far_count // 2)
+    def _():
+        pl.semaphore_wait(relay_sem, 2)
+        end = jnp.where(far == 0, next_ids[1], next_ids[0])
+        pl.semaphore_signal(relay_sem, inc=1, device_id={"row": end}, device_id_type=MESH)
+
     wait_received(recv1.at[pl.ds(0, NEAR - 1)], rs_sem)
     recv1[near] = send1[near]
     total = recv1[0].astype(F32)
@@ -276,12 +301,15 @@
         total = total + recv1[k].astype(F32)
     send2[...] = total.astype(BF16)
 
-    pl.semaphore_wait(relay_sem, len(next_ids))
+
+    @pl.when(far >= far_count // 2)
+    def _():
+        pl.semaphore_wait(relay_sem, 2)
+
     for k, other in sorted(enumerate(far_ids), key=lambda item: abs(2 * item[0] + 2 - far_count)):
         send(send2, recv2.at[k], far_sem, 1, other)
 
-    for k, (row, other) in enumerate([(rows_here - 1, below), (0, above)]):
-        send(tok.at[pl.ds(row * cols, cols)], halo.at[k], halo_sem, 1, other)
+    halo_rows(True)
 
     wait_received(recv2, far_sem)
     total = send2[...].astype(F32)

time: 51.2 us -> 51.1 us (level)
  no operation moved by 1% of the time
where the time goes in v5:
time: 51.1 us; the launch traced here: 51 us
  Pallas kernels  50.1 us (98%)
  local copies, waits for them, and re-layouts  0.88 us (2%)
    pallas_call x1, Pallas kernels, layer(): pl.pallas_call(functools.partial(kernel, n, heads), out_shape=jax.ShapeDt...  50.1 us

profile of v5, /device:TPU:33, one launch (start us, length us, event | category | flops | bytes accessed | tf_op | source)
XLA Modules:
  0.0 51.0 jit_solution(12306850800620487741)
XLA Ops:
  0.0 50.1 %favor_layer.1 = bf16[512,768]{1,0:T(8,128)(2,1)S(1)} custom-call(bf16[512,768]{1,0:T(8,128)(2,1)} %bitcast.3, bf16[768,768]{1,0:T(8,128)(2,1)} %wq_h.1, bf16[768,768]{1,0:T(8,128)(2,1)} %wk_h.1, bf16[768,768]{1,0:T(8,128)(2,1)} %wv_h.1, bf16[768,768]{1,0:T(8,128)(2,1)} %wo_h.1, bf16[12,64,256]{2,1,0:T(8,128)(2,1)} %om_h.1, f32[3,3,768]{2,1,0:T(4,128)} %ck_h.1, ...), custom_call_target="tpu_custom_call" | custom-call | tf_op jit(solution)/shard_map/favor_layer/pallas_call | solution.py:422
  50.1 0.9 %copy.10 = bf16[2,256,768]{2,1,0:T(8,128)(2,1)} copy(bf16[2,256,768]{2,1,0:T(8,128)(2,1)S(1)} %bitcast.2) | data formatting | bytes 1572864

commit v6 on v5

--- a/solution.py
+++ b/solution.py
@@ -294,6 +294,13 @@
         end = jnp.where(far == 0, next_ids[1], next_ids[0])
         pl.semaphore_signal(relay_sem, inc=1, device_id={"row": end}, device_id_type=MESH)
 
+    for half_of in range(2):
+        for p in range(pairs):
+            for i in range(2):
+                for s in range(2):
+                    rows = slice((2 * i + 1 - s) * dim_head, (2 * i + 2 - s) * dim_head)
+                    rhs[half_of, p, rows, s * half : (s + 1) * half] = jnp.zeros((dim_head, half), BF16)
+
     wait_received(recv1.at[pl.ds(0, NEAR - 1)], rs_sem)
     recv1[near] = send1[near]
     total = recv1[0].astype(F32)
@@ -355,7 +362,6 @@
         for source in sources:
             hand_on(slot(*source))
 
-    blank = jnp.zeros((dim_head, half), BF16)
 
     def operand(slot, h):
         for p in range(pairs):
@@ -371,22 +377,14 @@
                 sums.append(jnp.concatenate([key_sum] * (dim_head // (CHUNK - KV_ROWS)), axis=0))
             for s in range(2):
                 for i, block in enumerate([parts, sums]):
-                    for t in range(2):
-                        rhs[slot, p, (2 * i + t) * dim_head : (2 * i + t + 1) * dim_head, s * half : (s + 1) * half] = (
-                            block[s] if s == t else blank
-                        )
+                    rows = slice((2 * i + s) * dim_head, (2 * i + s + 1) * dim_head)
+                    rhs[slot, p, rows, s * half : (s + 1) * half] = block[s]
 
     operand(0, core)
     for p in range(pairs):
         at = slice(p * 2 * lanes, (p + 1) * 2 * lanes)
         partial[:, at] = dot_t(fq[core, :, at], rhs[0, p])
     wait_received(state.at[1 - core], fw_sem)
-    wait_sent(send0.at[1 - core], pair_sem)
-    wait_sent(send1.at[pl.ds(0, NEAR - 1)], rs_sem)
-    wait_sent(recv2, far_sem)
-    wait_sent(halo, halo_sem)
-    wait_sent(state.at[core, pl.ds(0, NEAR - 1)], ag_sem)
-    wait_sent(state.at[core], fw_sem)
     operand(1, 1 - core)
     gain_load.wait()
     o_load.wait()
@@ -408,6 +406,12 @@
             out[at, c : c + 256] = (
                 tok[at, c : c + 256].astype(F32) + dot(mixed[at], wo[:, c : c + 256])
             ).astype(BF16)
+    wait_sent(send0.at[1 - core], pair_sem)
+    wait_sent(send1.at[pl.ds(0, NEAR - 1)], rs_sem)
+    wait_sent(recv2, far_sem)
+    wait_sent(halo, halo_sem)
+    wait_sent(state.at[core, pl.ds(0, NEAR - 1)], ag_sem)
+    wait_sent(state.at[core], fw_sem)
 
 
 def layer(n, tokens, w_query, w_key, w_value, w_out, omega, conv_kernel, norm_gain):

time: 51.1 us -> 50.6 us (level)
  no operation moved by 1% of the time
where the time goes in v6:
time: 50.6 us; the launch traced here: 50.5 us
  Pallas kernels  49.6 us (98%)
  local copies, waits for them, and re-layouts  0.88 us (2%)
    pallas_call x1, Pallas kernels, layer(): pl.pallas_call(functools.partial(kernel, n, heads), out_shape=jax.ShapeDt...  49.6 us

profile of v6, /device:TPU:33, one launch (start us, length us, event | category | flops | bytes accessed | tf_op | source)
XLA Modules:
  0.0 50.5 jit_solution(14489360174239176456)
XLA Ops:
  0.0 49.6 %favor_layer.1 = bf16[512,768]{1,0:T(8,128)(2,1)S(1)} custom-call(bf16[512,768]{1,0:T(8,128)(2,1)} %bitcast.3, bf16[768,768]{1,0:T(8,128)(2,1)} %wq_h.1, bf16[768,768]{1,0:T(8,128)(2,1)} %wk_h.1, bf16[768,768]{1,0:T(8,128)(2,1)} %wv_h.1, bf16[768,768]{1,0:T(8,128)(2,1)} %wo_h.1, bf16[12,64,256]{2,1,0:T(8,128)(2,1)} %om_h.1, f32[3,3,768]{2,1,0:T(4,128)} %ck_h.1, ...), custom_call_target="tpu_custom_call" | custom-call | tf_op jit(solution)/shard_map/favor_layer/pallas_call | solution.py:426
  49.6 0.9 %copy.10 = bf16[2,256,768]{2,1,0:T(8,128)(2,1)} copy(bf16[2,256,768]{2,1,0:T(8,128)(2,1)S(1)} %bitcast.2) | data formatting | bytes 1572864
